TPU v7x, 32 devices: a whole 2x2x4 slice. The times are simulated.
32 devices in a mesh: tile: 8 (over z, x), sub: 4 (over y, core).
Axes of the slice: x: 2, y: 2, z: 4, core: 2. Of those that a mesh axis runs over, the one named last changes fastest.
Arguments:
- grid_feats: bfloat16 [4096, 512], P(('tile', 'sub')), may hold values from -6 to 6
- mesh_feats: bfloat16 [4096, 512], P(('tile', 'sub')), may hold values from -6 to 6
- encode_edges: bfloat16 [32768, 512], P(('tile', 'sub')), may hold values from -6 to 6
- decode_edges: bfloat16 [16384, 512], P(('tile', 'sub')), may hold values from -6 to 6
- encode_source: int32 [32768], P(('tile', 'sub')), may hold values from 0 to 4095, as said below
- encode_target: int32 [32768], P(('tile', 'sub')), may hold values from -1 to 4095, as said below
- decode_source: int32 [16384], P(('tile', 'sub')), may hold values from 0 to 4095, as said below
- decode_target: int32 [16384], P(('tile', 'sub')), may hold values from -1 to 4095, as said below
- owner_fine: int32 [4096], P(('tile', 'sub')), may hold values from 0 to 1023, as said below
- owner_coarse: int32 [1024], P('tile'), may hold values from 0 to 511
- encode_weight: bfloat16 [512, 512], replicated, may hold values from -0.25 to 0.25
- decode_weight: bfloat16 [512, 512], replicated, may hold values from -0.25 to 0.25
- middle_weight: bfloat16 [512, 512], replicated, may hold values from -0.25 to 0.25
- summit_weight: bfloat16 [512, 512], replicated, may hold values from -0.25 to 0.25
- cotangent: bfloat16 [4096, 512], P(('tile', 'sub')), may hold values from -6 to 6
Outputs:
- grid_update: bfloat16 [4096, 512], P(('tile', 'sub'))
- encode_grad: float32 [512, 512], replicated
- decode_grad: float32 [512, 512], replicated
- middle_grad: float32 [512, 512], replicated
- summit_grad: float32 [512, 512], replicated
Inputs may be any that keep to these rules, and one draw needn't show every extreme that they name: `encode_source`: edge slot e is listed on device d = e // 1024; its source grid node lies on device d - 1, d or d + 1. `encode_target`: -1 marks padding; every other value is a mesh node of the device that lists the slot. On each device padding fills whole blocks of 128 slots after all live ones; every device has a live block, and some device has no padding. `decode_source`: edge slot e is listed on device d = e // 512; its source mesh node lies on device d - 1, d or d + 1. `decode_target`: -1 marks padding; every other value is a grid node of the device that lists the slot. On each device padding fills whole blocks of 128 slots after all live ones; every device has a live block, and some device has no padding. `owner_fine`: the middle node of fine mesh node m lies on the tile of the device that holds m.
All inputs are finite; a program needn't handle non-finite values.
Results may differ from a plain program's by a relative error of at most 0.012.
Values may be sent and summed in bfloat16 or wider, within the bound.
No kernel may reach another device: no remote copies, remote signals or barrier semaphores. Data moves between devices by JAX's collectives and lax.ppermute only.
A program may use at most 64 MiB of HBM per device.

v0:
```python
import jax
import jax.numpy as jnp
from jax import lax
from jax.sharding import PartitionSpec as P

TOP_NODES = 512
BLOCK = 128


def extended(x, sides, width):
    for axis, dim in sides:
        peers, length = (lax.axis_size(axis), x.shape[dim])
        up = [(i, (i + 1) % peers) for i in range(peers - 1)]
        down = [(j, i) for i, j in up]
        last = lax.slice_in_dim(x, length - width, length, axis=dim)
        initial = lax.slice_in_dim(x, 0, width, axis=dim)
        before = lax.ppermute(last, axis, up)
        after = lax.ppermute(initial, axis, down)
        x = jnp.concatenate([before, x, after], axis=dim)
    return x


def from_behind(x, axis, by):
    peers = lax.axis_size(axis)
    pairs = [(i, i + by) for i in range(peers) if 0 <= i + by < peers]
    return lax.ppermute(x, axis, pairs)


def silu_slope(values):
    sigmoid = jax.nn.sigmoid(values)
    return sigmoid * (1.0 + values * (1.0 - sigmoid))


def live_count(targets):
    heads = targets.reshape(-1, BLOCK)[:, 0]
    return jnp.sum((heads >= 0).astype(jnp.int32))


def local_targets(targets, first, limit):
    return jnp.where(targets >= 0, targets - first, limit)


def outer_sum(left, right):
    return lax.dot_general(
        left, right, (((0,), (0,)), ((), ())), preferred_element_type=jnp.float32
    )


def times_transposed(left, right):
    return lax.dot_general(
        left, right, (((1,), (1,)), ((), ())), preferred_element_type=jnp.float32
    )


def membership(indices, rows, dtype):
    return (jnp.arange(rows, dtype=jnp.int32)[:, None] == indices[None, :]).astype(dtype)


def exact_sum(members, values):
    return jnp.dot(
        members, values, precision=lax.Precision.HIGHEST, preferred_element_type=jnp.float32
    )


def edge_forward(sources, senders, targets, edge_feats, weight, segments, blocks):
    features = weight.shape[1]

    def block_step(block_id, carried):
        summed, stored = carried
        offset = block_id * BLOCK
        picked = lax.dynamic_slice_in_dim(senders, offset, BLOCK)
        receivers = lax.dynamic_slice_in_dim(targets, offset, BLOCK)
        edge_part = lax.dynamic_slice_in_dim(edge_feats, offset, BLOCK, 0)
        fetched = jnp.take(sources, picked, axis=0)
        preact = jnp.dot(fetched, weight, preferred_element_type=jnp.float32) + edge_part.astype(
            jnp.float32
        )
        summed = summed + exact_sum(
            membership(receivers, segments, jnp.float32), jax.nn.silu(preact)
        )
        stored = lax.dynamic_update_slice_in_dim(stored, preact, offset, 0)
        return (summed, stored)

    start_sum = jnp.zeros((segments, features), jnp.float32)
    start_store = jnp.zeros((senders.shape[0], features), jnp.float32)
    return lax.fori_loop(0, blocks, block_step, (start_sum, start_store))


def edge_backward(
    sources, senders, targets, stored, weight, upstream, factor, blocks, returned_rows
):
    features = weight.shape[1]

    def block_step(block_id, carried):
        gradient, returned = carried
        offset = block_id * BLOCK
        picked = lax.dynamic_slice_in_dim(senders, offset, BLOCK)
        receivers = lax.dynamic_slice_in_dim(targets, offset, BLOCK)
        preact = lax.dynamic_slice_in_dim(stored, offset, BLOCK, 0)
        fetched = jnp.take(sources, picked, axis=0)
        incoming = jnp.take(upstream, receivers, axis=0).astype(jnp.float32) * factor
        slope = (incoming * silu_slope(preact)).astype(jnp.bfloat16)
        gradient = gradient + outer_sum(fetched, slope)
        if returned_rows:
            passed = times_transposed(slope, weight)
            returned = returned + exact_sum(membership(picked, returned_rows, jnp.float32), passed)
        return (gradient, returned)

    start_grad = jnp.zeros((features, features), jnp.float32)
    start_back = jnp.zeros((max(returned_rows, 1), features), jnp.float32)
    return lax.fori_loop(0, blocks, block_step, (start_grad, start_back))


def shards(
    grid_feats,
    mesh_feats,
    encode_edges,
    decode_edges,
    encode_source,
    encode_target,
    decode_source,
    decode_target,
    owner_fine,
    owner_coarse,
    encode_weight,
    decode_weight,
    middle_weight,
    summit_weight,
    cotangent,
):
    grid_rows = grid_feats.shape[0]
    mesh_rows = mesh_feats.shape[0]
    level_rows = owner_coarse.shape[0]
    tiles = lax.axis_size("tile")
    subs = lax.axis_size("sub")
    device = lax.axis_index(("tile", "sub"))
    tile_id = lax.axis_index("tile")
    encode_factor = mesh_rows / encode_source.shape[0]
    decode_factor = grid_rows / decode_source.shape[0]
    middle_factor = level_rows / (mesh_rows * subs)
    summit_factor = TOP_NODES / (level_rows * tiles)
    grid_wide = extended(grid_feats, ((("tile", "sub"), 0),), grid_rows)
    encode_senders = encode_source - (device - 1) * grid_rows
    encode_targets = local_targets(encode_target, device * mesh_rows, mesh_rows)
    encode_blocks = live_count(encode_target)
    encode_summed, encode_stored = edge_forward(
        grid_wide,
        encode_senders,
        encode_targets,
        encode_edges,
        encode_weight,
        mesh_rows,
        encode_blocks,
    )
    mesh_mid = (mesh_feats.astype(jnp.float32) + encode_factor * encode_summed).astype(jnp.bfloat16)
    fine_local = owner_fine - tile_id * level_rows
    fine_members = membership(fine_local, level_rows, jnp.bfloat16)
    middle_part = jnp.dot(fine_members, mesh_mid, preferred_element_type=jnp.float32)
    middle_sum = lax.psum(middle_part, "sub")
    middle_in = (middle_factor * middle_sum).astype(jnp.bfloat16)
    middle_act = jnp.dot(middle_in, middle_weight, preferred_element_type=jnp.float32)
    middle_out = (middle_in.astype(jnp.float32) + jax.nn.silu(middle_act)).astype(jnp.bfloat16)
    top_members = membership(owner_coarse, TOP_NODES, jnp.bfloat16)
    summit_part = jnp.dot(top_members, middle_out, preferred_element_type=jnp.float32)
    summit_whole = lax.psum(summit_part, "tile")
    summit_in = (summit_factor * summit_whole).astype(jnp.bfloat16)
    summit_act = jnp.dot(summit_in, summit_weight, preferred_element_type=jnp.float32)
    summit_out = jax.nn.silu(summit_act).astype(jnp.bfloat16)
    coarse_of = jnp.take(owner_coarse, fine_local)
    lifted = jnp.take(middle_out, fine_local, axis=0).astype(jnp.float32) + jnp.take(
        summit_out, coarse_of, axis=0
    ).astype(jnp.float32)
    mesh_out = (mesh_mid.astype(jnp.float32) + lifted).astype(jnp.bfloat16)
    mesh_wide = extended(mesh_out, ((("tile", "sub"), 0),), mesh_rows)
    decode_senders = decode_source - (device - 1) * mesh_rows
    decode_targets = local_targets(decode_target, device * grid_rows, grid_rows)
    decode_blocks = live_count(decode_target)
    decode_summed, decode_stored = edge_forward(
        mesh_wide,
        decode_senders,
        decode_targets,
        decode_edges,
        decode_weight,
        grid_rows,
        decode_blocks,
    )
    grid_update = (grid_feats.astype(jnp.float32) + decode_factor * decode_summed).astype(
        jnp.bfloat16
    )
    decode_local, decode_returned = edge_backward(
        mesh_wide,
        decode_senders,
        decode_targets,
        decode_stored,
        decode_weight,
        cotangent,
        decode_factor,
        decode_blocks,
        3 * mesh_rows,
    )
    from_next = from_behind(decode_returned[:mesh_rows], ("tile", "sub"), -1)
    from_prev = from_behind(decode_returned[2 * mesh_rows :], ("tile", "sub"), 1)
    mesh_grad = decode_returned[mesh_rows : 2 * mesh_rows] + from_next + from_prev
    level_part = exact_sum(fine_members.astype(jnp.float32), mesh_grad)
    level_grad = lax.psum(level_part, "sub")
    summit_grad_part = exact_sum(top_members.astype(jnp.float32), level_grad)
    summit_grad_whole = lax.psum(summit_grad_part, "tile")
    summit_slope = (summit_grad_whole * silu_slope(summit_act)).astype(jnp.bfloat16)
    summit_local = outer_sum(summit_in, summit_slope)
    summit_back = times_transposed(summit_slope, summit_weight).astype(jnp.bfloat16)
    level_total = level_grad + summit_factor * jnp.take(summit_back, owner_coarse, axis=0).astype(
        jnp.float32
    )
    middle_slope = (level_total * silu_slope(middle_act)).astype(jnp.bfloat16)
    middle_local = outer_sum(middle_in, middle_slope)
    middle_back = level_total + times_transposed(middle_slope, middle_weight)
    mesh_total = mesh_grad + middle_factor * jnp.take(middle_back, fine_local, axis=0)
    encode_local, unused_rows = edge_backward(
        grid_wide,
        encode_senders,
        encode_targets,
        encode_stored,
        encode_weight,
        mesh_total,
        encode_factor,
        encode_blocks,
        0,
    )
    sub_share = 1.0 / subs
    encode_grad, decode_grad, middle_grad = lax.psum(
        (encode_local, decode_local, sub_share * middle_local), ("tile", "sub")
    )
    return (grid_update, encode_grad, decode_grad, middle_grad, summit_local)


def solution(mesh):
    placed = (
        P(("tile", "sub"), None),
        P(("tile", "sub"), None),
        P(("tile", "sub"), None),
        P(("tile", "sub"), None),
        P(("tile", "sub")),
        P(("tile", "sub")),
        P(("tile", "sub")),
        P(("tile", "sub")),
        P(("tile", "sub")),
        P("tile"),
        P(),
        P(),
        P(),
        P(),
        P(("tile", "sub"), None),
    )
    return jax.shard_map(
        shards,
        mesh=mesh,
        in_specs=placed,
        out_specs=(P(("tile", "sub"), None), P(), P(), P(), P()),
        check_vma=False,
    )
```

profile of v0, /device:TPU:0, one launch (start us, length us, event | category | flops | bytes accessed | tf_op | source)
XLA Modules:
  0.0 564.3 jit_solution(5614955575473783883)
XLA Ops:
  7.2 2.5 collective-permute-start
  9.8 1.3 collective-permute-start.1
  12.5 1.3 convert_reduce_fusion
  15.4 1.6 broadcast_in_dim.93
  17.0 16.3 %while.46 = (s32[]{:T(128)}, f32[128,512]{1,0:T(8,128)S(1)}, f32[1024,512]{1,0:T(8,128)}, s32[]{:T(128)}, s32[1024]{0:T(1024)S(1)}, /*index=5*/s32[1024]{0:T(102...) while((s32[]{:T(128)}, f32[128,512]{1,0:T(8,128)S(1)}, ...), condition=%wide.region_3.5_spmd, body=%wide.region_2.0_spmd.sunk | while | flops 168314624 | bytes 2367415 | solution.py:86
  18.6 1.9 constant_dynamic-update-slice_fusion.7
  22.5 1.9 constant_dynamic-update-slice_fusion.7
  26.5 1.9 constant_dynamic-update-slice_fusion.7
  30.4 1.9 constant_dynamic-update-slice_fusion.7
  34.4 52.0 %all-reduce.7.cloned.1.call-done = f32[128,512]{1,0:T(8,128)} async-done(((f32[128,512]{1,0:T(8,128)}), f32[128,512]{1,0:T(8,128)}) %all-reduce.7.cloned.1.call-update) | async-done | bytes 262160 | tf_op jit(solution)/shard_map/psum | solution.py:159
  86.4 2.0 add_convert_fusion.2
  88.4 1.3 fusion.43
  91.9 76.8 %all-reduce.9.cloned.1.call-done = f32[512,512]{1,0:T(8,128)} async-done(((f32[512,512]{1,0:T(8,128)}), f32[512,512]{1,0:T(8,128)}) %all-reduce.9.cloned.1.call-update) | async-done | bytes 1048592 | tf_op jit(solution)/shard_map/psum | solution.py:165
  168.7 2.7 multiply_convert_fusion.6
  172.4 1.7 collective-permute-start.2
  174.1 1.3 collective-permute-start.3
  176.7 2.0 collective-permute-done.3
  179.6 19.5 %while.47 = (s32[]{:T(128)}, f32[128,512]{1,0:T(8,128)}, f32[512,512]{1,0:T(8,128)S(1)}, s32[]{:T(128)}, s32[512]{0:T(512)}, /*index=5*/s32[512]{0:T(512)}, bf16...) while((s32[]{:T(128)}, f32[128,512]{1,0:T(8,128)}, ...), condition=%wide.region_7.10_spmd, body=%wide.region_6.9_spmd.sunk | while | flops 168314624 | bytes 2367799 | solution.py:86
  183.9 2.0 convolution_add_fusion.14
  190.1 2.0 convolution_add_fusion.14
  196.4 2.0 convolution_add_fusion.14
  200.3 22.2 %while.48 = (s32[]{:T(128)}, f32[512,512]{1,0:T(8,128)S(1)}, f32[384,512]{1,0:T(8,128)S(1)}, s32[]{:T(128)}, s32[512]{0:T(512)}, /*index=5*/bf16[384,512]{1,0:T(...) while((s32[]{:T(128)}, f32[512,512]{1,0:T(8,128)S(1)}, ...), condition=%wide.region_9.12_spmd, body=%wide.region_8.11_spmd.sunk | while | flops 438357888 | bytes 8272603 | solution.py:111
  200.9 1.4 compare_and_fusion.16
  204.1 1.5 convolution_add_fusion.15
  205.6 1.3 fusion.84
  208.1 1.4 compare_and_fusion.16
  211.2 1.5 convolution_add_fusion.15
  212.8 1.3 fusion.84
  215.3 1.4 compare_and_fusion.16
  218.4 1.5 convolution_add_fusion.15
  220.0 1.3 fusion.84
  222.6 1.3 collective-permute-start.4
  223.9 6.1 %collective-permute-start.5 = (f32[128,512]{1,0:T(8,128)S(1)}, f32[128,512]{1,0:T(8,128)S(1)}, u32[]{:S(2)}, u32[]{:S(2)}) collective-permute-start(f32[128,512]{1,0:T(8,128)S(1)} %get-tuple-element.310), channel_id=1, source_target_pairs={{0,1},{1,2},{2,3},{3,4},{4,5},{5,6},{6,7},{7,8},{8,9},{9,10},{10,1... | collective-permute-start | bytes 786440 | tf_op jit(solution)/shard_map/ppermute | solution.py:26
  231.1 1.6 fusion.48
  232.8 53.1 %all-reduce.11.cloned.1.call-done = f32[128,512]{1,0:T(8,128)} async-done(((f32[128,512]{1,0:T(8,128)}), f32[128,512]{1,0:T(8,128)}) %all-reduce.11.cloned.1.call-update) | async-done | bytes 262160 | tf_op jit(solution)/shard_map/psum | solution.py:205
  285.9 2.5 fusion.42
  288.5 79.6 %all-reduce.13.cloned.1.call-done = f32[512,512]{1,0:T(8,128)} async-done(((f32[512,512]{1,0:T(8,128)}), f32[512,512]{1,0:T(8,128)}) %all-reduce.13.cloned.1.call-update) | async-done | bytes 1048592 | tf_op jit(solution)/shard_map/psum | solution.py:207
  368.1 1.9 multiply_convert_fusion.5
  371.4 1.6 convolution_add_fusion.7
  375.1 18.6 %while.49 = (s32[]{:T(128)}, f32[512,512]{1,0:T(8,128)S(1)}, s32[]{:T(128)}, s32[1024]{0:T(1024)}, bf16[384,512]{1,0:T(8,128)(2,1)S(1)}, /*index=5*/s32[1024]{0:...) while((s32[]{:T(128)}, f32[512,512]{1,0:T(8,128)S(1)}, ...), condition=%wide.region_13.16_spmd, body=%wide.region_12.15_spmd.sunk | while | flops 68161032 | bytes 3551915 | solution.py:111
  378.2 1.5 convolution_add_fusion.17
  382.6 1.5 convolution_add_fusion.17
  387.1 1.5 convolution_add_fusion.17
  391.6 1.5 convolution_add_fusion.17
  393.7 2.8 convolution_multiply_fusion
  398.2 2.7 fusion.44
  400.9 152.5 %all-reduce.15.cloned.1.call-done = (f32[512,512]{1,0:T(8,128)}, f32[512,512]{1,0:T(8,128)}, f32[512,512]{1,0:T(8,128)}) async-done(((f32[512,512]{1,0:T(8,128)}, f32[512,512]{1,0:T(8,128)}, f32[512,512]{1,0:T(8,128)}), (f32[512,512]{1,0:T(8,128)}, f32[512,512]{1,0:T(8,128)}, f32[512,512]{1,0:T(8,128)})) %all-reduce.15.cloned.1.call-update) | async-done | bytes 3145744 | tf_op jit(solution)/shard_map/psum | solution.py:230
  553.4 2.4 copy.68
  (179 shorter events, 51.6 us)
Async XLA Ops:
  7.2 161.6 %copy-start = (bf16[512,512]{1,0:T(8,128)(2,1)S(1)}, bf16[512,512]{1,0:T(8,128)(2,1)}, u32[]{:S(2)}) copy-start(bf16[512,512]{1,0:T(8,128)(2,1)} %param.40) | copy-start | bytes 1572868
  7.2 9.8 %copy-start.5 = (bf16[512,512]{1,0:T(8,128)(2,1)S(1)}, bf16[512,512]{1,0:T(8,128)(2,1)}, u32[]{:S(2)}) copy-start(bf16[512,512]{1,0:T(8,128)(2,1)} %param.37) | copy-start | bytes 1572868
  7.2 79.2 %all-reduce.7.cloned.1.call-start = ((), (), s32[]{:S(2)}) async-start(), calls=%async_computation | async-start | bytes 524288 | tf_op jit(solution)/shard_map/psum | solution.py:159
  7.2 6.5 %collective-permute-start = (bf16[128,512]{1,0:T(8,128)(2,1)}, bf16[128,512]{1,0:T(8,128)(2,1)S(1)}, u32[]{:S(2)}, u32[]{:S(2)}) collective-permute-start(bf16[128,512]{1,0:T(8,128)(2,1)} %param.27), channel_id=1, source_target_pairs={{0,1},{1,2},{2,3},{3,4},{4,5},{5,6},{6,7},{7,8},{8,9},{9,10},{10,1... | collective-permute-start | bytes 393224 | tf_op jit(solution)/shard_map/ppermute | solution.py:17
  9.8 5.6 collective-permute-start.1
  12.5 78.5 %copy-start.21 = (s32[128]{0:T(128)}, s32[128]{0:T(128)S(1)}, u32[]{:S(2)}) copy-start(s32[128]{0:T(128)S(1)} %get-tuple-element.300) | copy-start | bytes 1540
  17.0 16.4 %copy-start.14 = (bf16[128,512]{1,0:T(8,128)(2,1)S(1)}, bf16[128,512]{1,0:T(8,128)(2,1)}, u32[]{:S(2)}) copy-start(bf16[128,512]{1,0:T(8,128)(2,1)} %param.28) | copy-start | bytes 393220
  17.0 69.3 %copy-start.26 = (bf16[512,512]{1,0:T(8,128)(2,1)S(1)}, bf16[512,512]{1,0:T(8,128)(2,1)}, u32[]{:S(2)}) copy-start(bf16[512,512]{1,0:T(8,128)(2,1)} %param.39) | copy-start | bytes 1572868
  33.3 56.3 %copy-start.18 = (s32[1024]{0:T(1024)}, s32[1024]{0:T(1024)S(1)}, u32[]{:S(2)}) copy-start(s32[1024]{0:T(1024)S(1)} %get-tuple-element.780) | copy-start | bytes 12292
  33.4 56.3 %copy-start.19 = (s32[1024]{0:T(1024)}, s32[1024]{0:T(1024)S(1)}, u32[]{:S(2)}) copy-start(s32[1024]{0:T(1024)S(1)} %get-tuple-element.781) | copy-start | bytes 12292
  33.4 55.0 %copy-start.1 = (s32[128]{0:T(128)S(1)}, s32[128]{0:T(128)}, u32[]{:S(2)}) copy-start(s32[128]{0:T(128)} %param.36) | copy-start | bytes 1540
  34.3 134.4 %all-reduce.9.cloned.1.call-start = ((), (), s32[]{:S(2)}) async-start(), calls=%async_computation.1 | async-start | bytes 2097152 | tf_op jit(solution)/shard_map/psum | solution.py:165
  89.7 196.2 %all-reduce.11.cloned.1.call-start = ((), (), s32[]{:S(2)}) async-start(), calls=%async_computation.2 | async-start | bytes 524288 | tf_op jit(solution)/shard_map/psum | solution.py:205
  89.7 2.1 copy-start.22
  91.0 81.3 %copy-start.23 = (pred[128]{0:T(512)(128)(4,1)}, pred[128]{0:T(512)(128)(4,1)S(1)}, u32[]{:S(2)}) copy-start(pred[128]{0:T(512)(128)(4,1)S(1)} %get-tuple-element.298) | copy-start | bytes 388
  91.9 83.6 %copy-start.20 = (s32[512]{0:T(512)S(1)}, s32[512]{0:T(512)}, u32[]{:S(2)}) copy-start(s32[512]{0:T(512)} %param.34) | copy-start | bytes 6148
  91.9 83.6 %copy-start.25 = (s32[512]{0:T(512)S(1)}, s32[512]{0:T(512)}, u32[]{:S(2)}) copy-start(s32[512]{0:T(512)} %param.33) | copy-start | bytes 6148
  171.4 8.2 %copy-start.6 = (bf16[512,512]{1,0:T(8,128)(2,1)S(1)}, bf16[512,512]{1,0:T(8,128)(2,1)}, u32[]{:S(2)}) copy-start(bf16[512,512]{1,0:T(8,128)(2,1)} %param.38) | copy-start | bytes 1572868
  172.4 4.2 collective-permute-start.2
  174.1 4.6 collective-permute-start.3
  179.6 20.7 %copy-start.2 = (bf16[128,512]{1,0:T(8,128)(2,1)S(1)}, bf16[128,512]{1,0:T(8,128)(2,1)}, u32[]{:S(2)}) copy-start(bf16[128,512]{1,0:T(8,128)(2,1)} %param.41) | copy-start | bytes 393220
  199.1 1.0 copy-start.8
  204.0 1.5 copy-start.7
  211.2 1.5 copy-start.7
  218.4 1.5 copy-start.7
  222.5 65.9 %copy-start.3 = (f32[512,512]{1,0:T(8,128)}, f32[512,512]{1,0:T(8,128)S(1)}, u32[]{:S(2)}) copy-start(f32[512,512]{1,0:T(8,128)S(1)} %get-tuple-element.208) | copy-start | bytes 3145732
  222.6 7.4 %collective-permute-start.4 = (f32[128,512]{1,0:T(8,128)S(1)}, f32[128,512]{1,0:T(8,128)S(1)}, u32[]{:S(2)}, u32[]{:S(2)}) collective-permute-start(f32[128,512]{1,0:T(8,128)S(1)} %get-tuple-element.309), channel_id=1, source_target_pairs={{1,0},{2,1},{3,2},{4,3},{5,4},{6,5},{7,6},{8,7},{9,8},{10,9},{11,1... | collective-permute-start | bytes 786440 | tf_op jit(solution)/shard_map/ppermute | solution.py:26
  223.9 7.2 %collective-permute-start.5 = (f32[128,512]{1,0:T(8,128)S(1)}, f32[128,512]{1,0:T(8,128)S(1)}, u32[]{:S(2)}, u32[]{:S(2)}) collective-permute-start(f32[128,512]{1,0:T(8,128)S(1)} %get-tuple-element.310), channel_id=1, source_target_pairs={{0,1},{1,2},{2,3},{3,4},{4,5},{5,6},{6,7},{7,8},{8,9},{9,10},{10,1... | collective-permute-start | bytes 786440 | tf_op jit(solution)/shard_map/ppermute | solution.py:26
  231.1 138.9 %copy-start.11 = (f32[128,512]{1,0:T(8,128)}, f32[128,512]{1,0:T(8,128)S(1)}, u32[]{:S(2)}) copy-start(f32[128,512]{1,0:T(8,128)S(1)} %collective-permute-done.5) | copy-start | bytes 786436
  232.7 135.3 %all-reduce.13.cloned.1.call-start = ((), (), s32[]{:S(2)}) async-start(), calls=%async_computation.3 | async-start | bytes 2097152 | tf_op jit(solution)/shard_map/psum | solution.py:207
  288.4 264.9 %all-reduce.15.cloned.1.call-start = ((), (), s32[]{:S(2)}) async-start(), calls=%async_computation.4 | async-start | bytes 6291456 | tf_op jit(solution)/shard_map/psum | solution.py:230
  371.3 2.5 copy-start.16
  371.4 2.5 copy-start.24
  375.1 18.6 %copy-start.15 = (f32[128,512]{1,0:T(8,128)S(1)}, f32[128,512]{1,0:T(8,128)}, u32[]{:S(2)}) copy-start(f32[128,512]{1,0:T(8,128)} %all-reduce.11.cloned.1.call-done) | copy-start | bytes 786436
  375.1 18.6 %copy-start.17 = (bf16[128,512]{1,0:T(8,128)(2,1)S(1)}, bf16[128,512]{1,0:T(8,128)(2,1)}, u32[]{:S(2)}) copy-start(bf16[128,512]{1,0:T(8,128)(2,1)} %copy-done.16) | copy-start | bytes 393220
  393.7 2.8 copy-start.4
  396.5 0.9 copy-start.12
  396.5 1.0 copy-start.13
  553.4 2.4 copy-start.10
  553.4 3.4 copy-start.9
Sparse Core Ops, SparseCore 0:
  34.4 51.8 all-reduce.6
  90.4 78.2 all-reduce.8
  232.9 52.9 all-reduce.10
  289.8 78.2 all-reduce.12
  396.7 156.6 all-reduce.14
where the time goes:
time: 566 us; the launch traced here: 564 us
  waiting for transfers between devices  418 us (74%)
  matrix products  53.6 us (9%)
  local copies, waits for them, and re-layouts  34.9 us (6%)
  other arithmetic  17.7 us (3%)
  starting transfers between devices  14.4 us (3%)
  between operations  14.3 us (3%)
  loops' own time  11.6 us (2%)
    psum x1, waiting for transfers between devices, shards(): lax.psum((encode_local, decode_local, sub_share * middle_local), ('tile',...  152 us
    psum x1, waiting for transfers between devices, shards(): summit_grad_whole = lax.psum(summit_grad_part, 'tile')  79.6 us
    psum x1, waiting for transfers between devices, shards(): summit_whole = lax.psum(summit_part, 'tile')  76.8 us
    psum x1, waiting for transfers between devices, shards(): level_grad = lax.psum(level_part, 'sub')  53.1 us
    psum x1, waiting for transfers between devices, shards(): middle_sum = lax.psum(middle_part, 'sub')  52 us
    dot_general x9, matrix products, outer_sum(): lax.dot_general(left, right, (((0,), (0,)), ((), ())), preferred_element_...  16 us
    dot_general x12, matrix products, exact_sum(): jnp.dot(members, values, precision=lax.Precision.HIGHEST, preferred_eleme...  13.6 us
    gather x14, local copies, waits for them, and re-layouts, block_step(): fetched = jnp.take(sources, picked, axis=0)  11.9 us
  transfers between devices with their start and end apart: 11, of which 8 were waited for; matrix products, arithmetic and copies ran while one was open for 2% of the time, Pallas kernels for 0%

commit v1 on v0

--- a/solution.py
+++ b/solution.py
@@ -202,7 +202,21 @@
     from_prev = from_behind(decode_returned[2 * mesh_rows :], ("tile", "sub"), 1)
     mesh_grad = decode_returned[mesh_rows : 2 * mesh_rows] + from_next + from_prev
     level_part = exact_sum(fine_members.astype(jnp.float32), mesh_grad)
-    level_grad = lax.psum(level_part, "sub")
+
+    def meet_goods_now(payload):
+        which_axis = "sub"
+        num_devices = jax.lax.axis_size(which_axis)
+        main = payload
+        for dev in [
+            [(to_i, to_i ^ h) for to_i in range(num_devices)]
+            for h in (1, 2, 4, 8, 16)
+            if h < num_devices
+        ]:
+            opened = jax.lax.ppermute(main, axis_name=which_axis, perm=dev)
+            main = main + opened
+        return main
+
+    level_grad = meet_goods_now(level_part)
     summit_grad_part = exact_sum(top_members.astype(jnp.float32), level_grad)
     summit_grad_whole = lax.psum(summit_grad_part, "tile")
     summit_slope = (summit_grad_whole * silu_slope(summit_act)).astype(jnp.bfloat16)

time: 566 us -> 535 us (0.945)
  waiting for transfers between devices: 418 us -> 377 us
  starting transfers between devices: 14.4 us -> 30.3 us
  matrix products: 53.6 us -> 46.8 us
    psum x1 -> x0, waiting for transfers between devices: 53.1 us -> none  [shards(): level_grad = lax.psum(level_part, 'sub')]
    ppermute x0 -> x2, starting transfers between devices: none -> 15.9 us  [meet_goods_now(): opened = jax.lax.ppermute(main, axis_name=which_axis, perm=dev)]
    ppermute x0 -> x2, waiting for transfers between devices: none -> 8 us  [meet_goods_now(): opened = jax.lax.ppermute(main, axis_name=which_axis, perm=dev)]
    dot_general x12, matrix products: 13.6 us -> 7.13 us  [exact_sum(): jnp.dot(members, values, precision=lax.Precision.HIGHEST, preferred_eleme...]
  transfers between devices with their start and end apart: 11 -> 12, of which waited for: 8 -> 9; matrix products, arithmetic and copies ran while one was open for 2% -> 2% of each run, Pallas kernels for 0% -> 0%
where the time goes in v1:
time: 535 us; the launch traced here: 534 us
  waiting for transfers between devices  377 us (70%)
  matrix products  46.8 us (9%)
  local copies, waits for them, and re-layouts  34.8 us (7%)
  starting transfers between devices  30.3 us (6%)
  other arithmetic  17.8 us (3%)
  between operations  14.3 us (3%)
  loops' own time  12.1 us (2%)
    psum x1, waiting for transfers between devices, shards(): lax.psum((encode_local, decode_local, sub_share * middle_local), ('tile',...  153 us
    psum x1, waiting for transfers between devices, shards(): summit_grad_whole = lax.psum(summit_grad_part, 'tile')  83.3 us
    psum x1, waiting for transfers between devices, shards(): summit_whole = lax.psum(summit_part, 'tile')  76.8 us
    psum x1, waiting for transfers between devices, shards(): middle_sum = lax.psum(middle_part, 'sub')  52.6 us
    dot_general x9, matrix products, outer_sum(): lax.dot_general(left, right, (((0,), (0,)), ((), ())), preferred_element_...  16 us
    ppermute x2, starting transfers between devices, meet_goods_now(): opened = jax.lax.ppermute(main, axis_name=which_axis, perm=dev)  15.9 us
    gather x14, local copies, waits for them, and re-layouts, block_step(): fetched = jnp.take(sources, picked, axis=0)  11.9 us
    dot_general x7, matrix products, block_step(): jnp.dot(fetched, weight, preferred_element_type=jnp.float32)  11.2 us
  transfers between devices with their start and end apart: 12, of which 9 were waited for; matrix products, arithmetic and copies ran while one was open for 2% of the time, Pallas kernels for 0%

profile of v1, /device:TPU:0, one launch (start us, length us, event | category | flops | bytes accessed | tf_op | source)
XLA Modules:
  0.0 533.6 jit_solution(1008872622091899692)
XLA Ops:
  7.2 2.5 collective-permute-start
  9.8 1.3 collective-permute-start.1
  12.5 1.4 convert_reduce_fusion
  15.4 1.6 broadcast_in_dim.93
  17.0 16.9 %while.46 = (s32[]{:T(128)}, f32[128,512]{1,0:T(8,128)S(1)}, f32[1024,512]{1,0:T(8,128)}, s32[]{:T(128)}, s32[1024]{0:T(1024)S(1)}, /*index=5*/s32[1024]{0:T(102...) while((s32[]{:T(128)}, f32[128,512]{1,0:T(8,128)S(1)}, ...), condition=%wide.region_3.5_spmd, body=%wide.region_2.0_spmd.sunk | while | flops 168314624 | bytes 2367415 | solution.py:86
  18.7 1.9 constant_dynamic-update-slice_fusion.7
  22.8 1.9 constant_dynamic-update-slice_fusion.7
  26.8 1.9 constant_dynamic-update-slice_fusion.7
  30.8 1.9 constant_dynamic-update-slice_fusion.7
  34.9 52.6 %all-reduce.6.cloned.1.call-done = f32[128,512]{1,0:T(8,128)} async-done(((f32[128,512]{1,0:T(8,128)}), f32[128,512]{1,0:T(8,128)}) %all-reduce.6.cloned.1.call-update) | async-done | bytes 262160 | tf_op jit(solution)/shard_map/psum | solution.py:159
  87.6 2.0 add_convert_fusion.2
  89.5 1.3 fusion.43
  90.9 1.2 gather_fusion.7
  93.1 76.8 %all-reduce.8.cloned.1.call-done = f32[512,512]{1,0:T(8,128)} async-done(((f32[512,512]{1,0:T(8,128)}), f32[512,512]{1,0:T(8,128)}) %all-reduce.8.cloned.1.call-update) | async-done | bytes 1048592 | tf_op jit(solution)/shard_map/psum | solution.py:165
  169.9 2.7 multiply_convert_fusion.6
  173.6 1.7 collective-permute-start.2
  175.3 1.3 collective-permute-start.3
  177.9 2.0 collective-permute-done.3
  180.1 14.3 %while.47 = (s32[]{:T(128)}, f32[128,512]{1,0:T(8,128)S(1)}, f32[512,512]{1,0:T(8,128)S(1)}, s32[]{:T(128)}, s32[512]{0:T(512)}, /*index=5*/s32[512]{0:T(512)}, ...) while((s32[]{:T(128)}, f32[128,512]{1,0:T(8,128)S(1)}, ...), condition=%wide.region_7.10_spmd, body=%wide.region_6.9_spmd.sunk | while | flops 168314624 | bytes 2367799 | solution.py:86
  182.3 1.2 constant_dynamic-update-slice_fusion.8
  196.3 21.6 %while.48 = (s32[]{:T(128)}, f32[512,512]{1,0:T(8,128)S(1)}, f32[384,512]{1,0:T(8,128)S(1)}, s32[]{:T(128)}, s32[512]{0:T(512)}, /*index=5*/bf16[384,512]{1,0:T(...) while((s32[]{:T(128)}, f32[512,512]{1,0:T(8,128)S(1)}, ...), condition=%wide.region_9.12_spmd, body=%wide.region_8.11_spmd.sunk | while | flops 438357888 | bytes 8272603 | solution.py:111
  196.9 1.3 compare_and_fusion.16
  199.9 1.5 convolution_add_fusion.15
  201.4 1.3 fusion.84
  203.9 1.3 compare_and_fusion.16
  206.9 1.5 convolution_add_fusion.15
  208.5 1.3 fusion.84
  210.9 1.3 compare_and_fusion.16
  214.0 1.5 convolution_add_fusion.15
  215.5 1.3 fusion.84
  218.0 1.3 collective-permute-start.4
  219.3 6.1 %collective-permute-start.5 = (f32[128,512]{1,0:T(8,128)S(1)}, f32[128,512]{1,0:T(8,128)S(1)}, u32[]{:S(2)}, u32[]{:S(2)}) collective-permute-start(f32[128,512]{1,0:T(8,128)S(1)} %get-tuple-element.310), channel_id=1, source_target_pairs={{0,1},{1,2},{2,3},{3,4},{4,5},{5,6},{6,7},{7,8},{8,9},{9,10},{10,1... | collective-permute-start | bytes 786440 | tf_op jit(solution)/shard_map/ppermute | solution.py:26
  227.5 3.9 collective-permute-start.6
  232.6 12.0 %collective-permute-start.7 = (f32[128,512]{1,0:T(8,128)S(1)}, f32[128,512]{1,0:T(8,128)S(1)}, u32[]{:S(2)}, u32[]{:S(2)}) collective-permute-start(f32[128,512]{1,0:T(8,128)S(1)} %add.198), channel_id=1, source_target_pairs={{0,2},{1,3},{2,0},{3,1},{4,6},{5,7},{6,4},{7,5},{8,10},{9,11},{10,... | collective-permute-start | bytes 786440 | tf_op jit(solution)/shard_map/ppermute | solution.py:215
  244.6 6.8 %collective-permute-done.7 = f32[128,512]{1,0:T(8,128)S(1)} collective-permute-done((f32[128,512]{1,0:T(8,128)S(1)}, f32[128,512]{1,0:T(8,128)S(1)}, u32[]{:S(2)}, u32[]{:S(2)}) %collective-permute-start.7) | collective-permute-done | bytes 262176 | tf_op jit(solution)/shard_map/ppermute | solution.py:215
  251.5 1.6 fusion.42
  253.2 83.3 %all-reduce.10.cloned.1.call-done = f32[512,512]{1,0:T(8,128)} async-done(((f32[512,512]{1,0:T(8,128)}), f32[512,512]{1,0:T(8,128)}) %all-reduce.10.cloned.1.call-update) | async-done | bytes 1048592 | tf_op jit(solution)/shard_map/psum | solution.py:221
  336.5 2.0 multiply_convert_fusion.5
  339.8 1.4 convolution_add_fusion.7
  343.3 19.2 %while.49 = (s32[]{:T(128)}, f32[512,512]{1,0:T(8,128)S(1)}, s32[]{:T(128)}, s32[1024]{0:T(1024)}, bf16[384,512]{1,0:T(8,128)(2,1)S(1)}, /*index=5*/s32[1024]{0:...) while((s32[]{:T(128)}, f32[512,512]{1,0:T(8,128)S(1)}, ...), condition=%wide.region_12.15_spmd, body=%wide.region_11.14_spmd.sunk | while | flops 68161032 | bytes 3551915 | solution.py:111
  346.4 1.5 convolution_add_fusion.17
  351.0 1.5 convolution_add_fusion.17
  355.7 1.5 convolution_add_fusion.17
  360.3 1.5 convolution_add_fusion.17
  362.5 2.8 convolution_multiply_fusion
  367.0 2.7 fusion.44
  369.7 153.0 %all-reduce.12.cloned.1.call-done = (f32[512,512]{1,0:T(8,128)}, f32[512,512]{1,0:T(8,128)}, f32[512,512]{1,0:T(8,128)}) async-done(((f32[512,512]{1,0:T(8,128)}, f32[512,512]{1,0:T(8,128)}, f32[512,512]{1,0:T(8,128)}), (f32[512,512]{1,0:T(8,128)}, f32[512,512]{1,0:T(8,128)}, f32[512,512]{1,0:T(8,128)})) %all-reduce.12.cloned.1.call-update) | async-done | bytes 3145744 | tf_op jit(solution)/shard_map/psum | solution.py:244
  522.7 2.4 copy.67
  (182 shorter events, 52.5 us)
Async XLA Ops:
  7.2 162.8 %copy-start = (bf16[512,512]{1,0:T(8,128)(2,1)S(1)}, bf16[512,512]{1,0:T(8,128)(2,1)}, u32[]{:S(2)}) copy-start(bf16[512,512]{1,0:T(8,128)(2,1)} %param.40) | copy-start | bytes 1572868
  7.2 9.8 %copy-start.5 = (bf16[512,512]{1,0:T(8,128)(2,1)S(1)}, bf16[512,512]{1,0:T(8,128)(2,1)}, u32[]{:S(2)}) copy-start(bf16[512,512]{1,0:T(8,128)(2,1)} %param.37) | copy-start | bytes 1572868
  7.2 80.4 %all-reduce.6.cloned.1.call-start = ((), (), s32[]{:S(2)}) async-start(), calls=%async_computation | async-start | bytes 524288 | tf_op jit(solution)/shard_map/psum | solution.py:159
  7.2 6.6 %collective-permute-start = (bf16[128,512]{1,0:T(8,128)(2,1)}, bf16[128,512]{1,0:T(8,128)(2,1)S(1)}, u32[]{:S(2)}, u32[]{:S(2)}) collective-permute-start(bf16[128,512]{1,0:T(8,128)(2,1)} %param.27), channel_id=1, source_target_pairs={{0,1},{1,2},{2,3},{3,4},{4,5},{5,6},{6,7},{7,8},{8,9},{9,10},{10,1... | collective-permute-start | bytes 393224 | tf_op jit(solution)/shard_map/ppermute | solution.py:17
  9.8 5.6 %collective-permute-start.1 = (bf16[128,512]{1,0:T(8,128)(2,1)}, bf16[128,512]{1,0:T(8,128)(2,1)S(1)}, u32[]{:S(2)}, u32[]{:S(2)}) collective-permute-start(bf16[128,512]{1,0:T(8,128)(2,1)} %param.27), channel_id=1, source_target_pairs={{1,0},{2,1},{3,2},{4,3},{5,4},{6,5},{7,6},{8,7},{9,8},{10,9},{11,1... | collective-permute-start | bytes 393224 | tf_op jit(solution)/shard_map/ppermute | solution.py:18
  12.5 79.7 %copy-start.20 = (s32[128]{0:T(128)}, s32[128]{0:T(128)S(1)}, u32[]{:S(2)}) copy-start(s32[128]{0:T(128)S(1)} %get-tuple-element.300) | copy-start | bytes 1540
  17.0 16.9 %copy-start.16 = (bf16[128,512]{1,0:T(8,128)(2,1)S(1)}, bf16[128,512]{1,0:T(8,128)(2,1)}, u32[]{:S(2)}) copy-start(bf16[128,512]{1,0:T(8,128)(2,1)} %param.28) | copy-start | bytes 393220
  17.0 70.5 %copy-start.25 = (bf16[512,512]{1,0:T(8,128)(2,1)S(1)}, bf16[512,512]{1,0:T(8,128)(2,1)}, u32[]{:S(2)}) copy-start(bf16[512,512]{1,0:T(8,128)(2,1)} %param.39) | copy-start | bytes 1572868
  33.9 56.9 %copy-start.17 = (s32[1024]{0:T(1024)}, s32[1024]{0:T(1024)S(1)}, u32[]{:S(2)}) copy-start(s32[1024]{0:T(1024)S(1)} %get-tuple-element.780) | copy-start | bytes 12292
  33.9 56.9 %copy-start.18 = (s32[1024]{0:T(1024)}, s32[1024]{0:T(1024)S(1)}, u32[]{:S(2)}) copy-start(s32[1024]{0:T(1024)S(1)} %get-tuple-element.781) | copy-start | bytes 12292
  33.9 55.6 %copy-start.1 = (s32[128]{0:T(128)S(1)}, s32[128]{0:T(128)}, u32[]{:S(2)}) copy-start(s32[128]{0:T(128)} %param.36) | copy-start | bytes 1540
  34.9 135.0 %all-reduce.8.cloned.1.call-start = ((), (), s32[]{:S(2)}) async-start(), calls=%async_computation.1 | async-start | bytes 2097152 | tf_op jit(solution)/shard_map/psum | solution.py:165
  90.8 245.6 %all-reduce.10.cloned.1.call-start = ((), (), s32[]{:S(2)}) async-start(), calls=%async_computation.2 | async-start | bytes 2097152 | tf_op jit(solution)/shard_map/psum | solution.py:221
  90.9 81.7 %copy-start.21 = (s32[1024]{0:T(1024)}, s32[1024]{0:T(1024)S(1)}, u32[]{:S(2)}) copy-start(s32[1024]{0:T(1024)S(1)} %pad_clamp_fusion.8) | copy-start | bytes 12292
  92.2 81.3 %copy-start.22 = (pred[128]{0:T(512)(128)(4,1)}, pred[128]{0:T(512)(128)(4,1)S(1)}, u32[]{:S(2)}) copy-start(pred[128]{0:T(512)(128)(4,1)S(1)} %get-tuple-element.298) | copy-start | bytes 388
  93.1 83.6 %copy-start.19 = (s32[512]{0:T(512)S(1)}, s32[512]{0:T(512)}, u32[]{:S(2)}) copy-start(s32[512]{0:T(512)} %param.34) | copy-start | bytes 6148
  93.1 83.6 %copy-start.24 = (s32[512]{0:T(512)S(1)}, s32[512]{0:T(512)}, u32[]{:S(2)}) copy-start(s32[512]{0:T(512)} %param.33) | copy-start | bytes 6148
  172.6 7.4 %copy-start.6 = (bf16[512,512]{1,0:T(8,128)(2,1)S(1)}, bf16[512,512]{1,0:T(8,128)(2,1)}, u32[]{:S(2)}) copy-start(bf16[512,512]{1,0:T(8,128)(2,1)} %param.38) | copy-start | bytes 1572868
  173.6 4.2 collective-permute-start.2
  175.3 4.6 collective-permute-start.3
  180.1 16.2 %copy-start.2 = (bf16[128,512]{1,0:T(8,128)(2,1)S(1)}, bf16[128,512]{1,0:T(8,128)(2,1)}, u32[]{:S(2)}) copy-start(bf16[128,512]{1,0:T(8,128)(2,1)} %param.41) | copy-start | bytes 393220
  194.4 1.0 copy-start.8
  195.4 0.7 copy-start.13
  199.9 1.5 copy-start.7
  206.9 1.5 copy-start.7
  213.9 1.5 copy-start.7
  217.9 35.1 %copy-start.3 = (f32[512,512]{1,0:T(8,128)}, f32[512,512]{1,0:T(8,128)S(1)}, u32[]{:S(2)}) copy-start(f32[512,512]{1,0:T(8,128)S(1)} %get-tuple-element.208) | copy-start | bytes 3145732
  218.0 7.4 %collective-permute-start.4 = (f32[128,512]{1,0:T(8,128)S(1)}, f32[128,512]{1,0:T(8,128)S(1)}, u32[]{:S(2)}, u32[]{:S(2)}) collective-permute-start(f32[128,512]{1,0:T(8,128)S(1)} %get-tuple-element.309), channel_id=1, source_target_pairs={{1,0},{2,1},{3,2},{4,3},{5,4},{6,5},{7,6},{8,7},{9,8},{10,9},{11,1... | collective-permute-start | bytes 786440 | tf_op jit(solution)/shard_map/ppermute | solution.py:26
  219.3 7.2 %collective-permute-start.5 = (f32[128,512]{1,0:T(8,128)S(1)}, f32[128,512]{1,0:T(8,128)S(1)}, u32[]{:S(2)}, u32[]{:S(2)}) collective-permute-start(f32[128,512]{1,0:T(8,128)S(1)} %get-tuple-element.310), channel_id=1, source_target_pairs={{0,1},{1,2},{2,3},{3,4},{4,5},{5,6},{6,7},{7,8},{8,9},{9,10},{10,1... | collective-permute-start | bytes 786440 | tf_op jit(solution)/shard_map/ppermute | solution.py:26
  225.4 6.0 %copy-start.11 = (f32[128,512]{1,0:T(8,128)}, f32[128,512]{1,0:T(8,128)S(1)}, u32[]{:S(2)}) copy-start(f32[128,512]{1,0:T(8,128)S(1)} %collective-permute-done.4) | copy-start | bytes 786436
  226.5 26.6 %copy-start.12 = (f32[128,512]{1,0:T(8,128)}, f32[128,512]{1,0:T(8,128)S(1)}, u32[]{:S(2)}) copy-start(f32[128,512]{1,0:T(8,128)S(1)} %collective-permute-done.5) | copy-start | bytes 786436
  227.5 5.1 collective-permute-start.6
  232.6 18.8 %collective-permute-start.7 = (f32[128,512]{1,0:T(8,128)S(1)}, f32[128,512]{1,0:T(8,128)S(1)}, u32[]{:S(2)}, u32[]{:S(2)}) collective-permute-start(f32[128,512]{1,0:T(8,128)S(1)} %add.198), channel_id=1, source_target_pairs={{0,2},{1,3},{2,0},{3,1},{4,6},{5,7},{6,4},{7,5},{8,10},{9,11},{10,... | collective-permute-start | bytes 786440 | tf_op jit(solution)/shard_map/ppermute | solution.py:215
  253.1 269.6 %all-reduce.12.cloned.1.call-start = ((), (), s32[]{:S(2)}) async-start(), calls=%async_computation.3 | async-start | bytes 6291456 | tf_op jit(solution)/shard_map/psum | solution.py:244
  336.4 3.3 copy-start.26
  339.7 2.3 copy-start.23
  362.5 2.8 copy-start.4
  365.3 0.9 copy-start.14
  365.3 1.0 copy-start.15
  522.7 2.4 copy-start.10
  522.7 3.4 copy-start.9
Sparse Core Ops, SparseCore 0:
  35.0 52.5 all-reduce.5
  91.6 78.2 all-reduce.7
  253.2 83.1 all-reduce.9
  365.5 157.1 all-reduce.11
